TPU v7x, 32 devices: a whole 2x2x4 slice. The times are simulated.
32 devices in a mesh: slab: 16 (over z, y, x), comp: 2 (over core).
Axes of the slice: x: 2, y: 2, z: 4, core: 2. Of those that a mesh axis runs over, the one named last changes fastest.
Arguments:
- polarization: float32 [6, 16, 128, 128], P('comp', 'slab'), parts along dimension 0, may hold values from -6 to 6
- inverse_polarizability: float32 [16, 128, 128], P('slab'), may hold values from 0.5 to 2
- occupancy: int32 [16, 16, 16], P('slab'), may hold values 0 or 1
- green_fourier: float32 [6, 256, 32, 256], P(None, 'slab'), may hold values from -12 to 12
Outputs:
- first_image: float32 [6, 16, 128, 128], P('comp', 'slab'), parts along dimension 0
- second_image: float32 [6, 16, 128, 128], P('comp', 'slab'), parts along dimension 0
There are 2 independent parts, one for each index of `comp`. A program takes and returns all parts, laid end to end along the dimension named above; an argument that names none is the same for every part. Nothing has to cross between parts.
All inputs are finite; a program needn't handle non-finite values. No bound on the sum of `occupancy` on one device may be relied on, other than what follows from the above.
Results may differ from a plain program's by a relative error of at most 0.0001.
Values sent between devices are 32-bit elements; how exact they have to be, the bound alone decides.
A program may use at most 64 MiB of HBM per device.

v0:
```python
import functools
import math

import jax
import jax.numpy as jnp
import numpy as np
from jax import lax
from jax.experimental import pallas as pl
from jax.experimental.pallas import tpu as pltpu
from jax.sharding import PartitionSpec as P

BLOCK = 8
MATVECS = 2
F32 = jnp.float32
BF16 = jnp.bfloat16
COMBOS = ((0, 3, 4), (3, 1, 5), (4, 5, 2))


def tables(count_in, count_out, length):
    phase = np.arange(count_in)[:, None] * np.arange(count_out)[None, :] % length
    angle = phase * (2.0 * math.pi / length)
    return np.cos(angle), np.sin(angle)


def split_table(table):
    table = table.astype(np.float32)
    high = table.astype(jnp.bfloat16)
    low = (table - high.astype(np.float32)).astype(jnp.bfloat16)
    return high, low


def split(value):
    high = value.astype(BF16)
    return high, (value - high.astype(F32)).astype(BF16)


def twiddle(re, im, num, length, sign):
    num = num * sign % length
    if num == 0:
        return re, im
    if 4 * num == length:
        return -im, re
    if 2 * num == length:
        return -re, -im
    if 4 * num == 3 * length:
        return im, -re
    c = math.cos(2.0 * math.pi * num / length)
    s = math.sin(2.0 * math.pi * num / length)
    if (8 * num) % length == 0:
        a = abs(c)
        p, m = (re + im) * a, (re - im) * a
        return {1: (m, p), 3: (-p, m), 5: (-m, -p), 7: (p, -m)}[8 * num // length]
    return re * c - im * s, re * s + im * c


def fft(values, sign):
    n = len(values)
    if n == 1:
        return values
    even, odd = fft(values[0::2], sign), fft(values[1::2], sign)
    low, high = [], []
    for k in range(n // 2):
        (er, ei), (o_r, oi) = even[k], twiddle(*odd[k], k, n, sign)
        low.append((er + o_r, ei + oi))
        high.append((er - o_r, ei - oi))
    return low + high


def three_pass(pair, table_pair, dims):
    dot = functools.partial(lax.dot_general, dimension_numbers=dims, preferred_element_type=F32)
    (vh, vl), (th, tl) = pair, table_pair
    return dot(vh, th) + (dot(vl, th) + dot(vh, tl))


def kernel(
    n, cells_x, padded_x, kz_own, kc,
    pol_ref, inv_ref, occ_ref, green_ref, wz_h, wz_l, wy_h, wy_l, vy_h, vy_l, vz_h, vz_l,
    first_ref, second_ref,
    green_raw, green, mask_ref, out_t, in_t, spec, fld, out_u, in_u,
    green_sem, fs_sem, fr_sem, is_sem, ir_sem,
):
    me = lax.axis_index("slab")
    chunks = kz_own // kc
    cells_y, cells_z = mask_ref.shape
    padded_y = 2 * cells_y
    halves = padded_y // 128
    green_copy = pltpu.make_async_copy(green_ref, green_raw, green_sem)
    green_copy.start()

    barrier = pltpu.get_barrier_semaphore()

    def greet(k, carry):
        pl.semaphore_signal(
            barrier, inc=1, device_id={"slab": lax.rem(me + k, n)}, device_id_type=pl.DeviceIdType.MESH
        )
        return carry

    lax.fori_loop(1, n, greet, 0)

    blocks_y, blocks_z = occ_ref.shape[1:]
    up_y = lax.broadcasted_iota(jnp.int32, (cells_y, blocks_y), 0) // BLOCK
    up_y = (up_y == lax.broadcasted_iota(jnp.int32, (cells_y, blocks_y), 1)).astype(F32).astype(BF16)
    up_z = lax.broadcasted_iota(jnp.int32, (blocks_z, cells_z), 1) // BLOCK
    up_z = (up_z == lax.broadcasted_iota(jnp.int32, (blocks_z, cells_z), 0)).astype(F32).astype(BF16)
    flags = occ_ref[0].astype(F32).astype(BF16)
    spread = jnp.dot(up_y, flags, preferred_element_type=F32).astype(BF16)
    mask_ref[...] = jnp.dot(spread, up_z, preferred_element_type=F32)

    def forward_z(c, field):
        pair = split(field)
        for part in range(2):
            rows = slice(part * 2 * cells_z, (part + 1) * 2 * cells_z)
            dims = (((1,), (1,)), ((), ()))
            res = three_pass((wz_h[rows, :], wz_l[rows, :]), pair, dims)
            out_t[:, 2 * c + part] = res.reshape(n, kz_own, cells_y)

    def block(ref, index, j):
        return ref.at[index, :, pl.ds(j * kc, kc), :]

    def exchange(source, target, j, send_sem, recv_sem):
        def send(k, carry):
            peer = lax.rem(me + k, n)
            pltpu.make_async_remote_copy(
                src_ref=block(source, peer, j),
                dst_ref=block(target, me, j),
                send_sem=send_sem,
                recv_sem=recv_sem,
                device_id={"slab": peer},
                device_id_type=pl.DeviceIdType.MESH,
            ).start()
            return carry

        lax.fori_loop(1, n, send, 0)
        target[me, :, j * kc:(j + 1) * kc, :] = source[me, :, j * kc:(j + 1) * kc, :]

    def drain(ref, sem, j):
        view = ref.at[pl.ds(0, n - 1), :, pl.ds(j * kc, kc), :]
        pltpu.make_async_copy(view, view, sem).wait()

    def order_green():
        green_copy.wait()

        def one(g, carry):
            for j in range(chunks):
                for t in range(0, padded_x, 8):
                    tile = green_raw[g, j * kc:(j + 1) * kc, t:t + 8, :]
                    tile = jnp.swapaxes(tile, 0, 1)
                    for h in range(halves):
                        green[j, h, g, t:t + 8] = tile[:, :, h * 128:(h + 1) * 128]
            return carry

        lax.fori_loop(0, 6, one, 0)

    def middle(j):
        dims = (((1,), (0,)), ((), ()))
        for c in range(3):
            re = in_t[:, 2 * c, j * kc:(j + 1) * kc, :].reshape(cells_x * kc, cells_y)
            im = in_t[:, 2 * c + 1, j * kc:(j + 1) * kc, :].reshape(cells_x * kc, cells_y)
            pair = split(jnp.concatenate([re, im], axis=1))
            res = three_pass(pair, (wy_h[...], wy_l[...]), dims)
            for part in range(2):
                for h in range(halves):
                    at = part * padded_y + h * 128
                    spec[h, 2 * c + part] = res[:, at:at + 128].reshape(cells_x, kc, 128)

        def columns(h, carry):
            for c in range(3):
                line = [(spec[h, 2 * c, x], spec[h, 2 * c + 1, x]) for x in range(cells_x)]
                for m, (re, im) in enumerate(fft(line, -1)):
                    fld[2 * c, 2 * m], fld[2 * c + 1, 2 * m] = re, im
                line = [twiddle(*line[x], x, padded_x, -1) for x in range(cells_x)]
                for m, (re, im) in enumerate(fft(line, -1)):
                    fld[2 * c, 2 * m + 1], fld[2 * c + 1, 2 * m + 1] = re, im
            for kx in range(padded_x):
                g = [green[j, h, i, kx] for i in range(6)]
                for part in range(2):
                    s = [fld[2 * b + part, kx] for b in range(3)]
                    for a, row in enumerate(COMBOS):
                        fld[2 * a + part, kx] = g[row[0]] * s[0] + g[row[1]] * s[1] + g[row[2]] * s[2]
            for a in range(3):
                even = fft([(fld[2 * a, k], fld[2 * a + 1, k]) for k in range(0, padded_x, 2)], 1)
                for x in range(cells_x):
                    spec[h, 2 * a, x], spec[h, 2 * a + 1, x] = even[x]
                odd = fft([(fld[2 * a, k], fld[2 * a + 1, k]) for k in range(1, padded_x, 2)], 1)
                for x in range(cells_x):
                    re, im = twiddle(*odd[x], x, padded_x, 1)
                    spec[h, 2 * a, x] += re
                    spec[h, 2 * a + 1, x] += im
            return carry

        lax.fori_loop(0, halves, columns, 0)
        for a in range(3):
            parts = [
                spec[h, 2 * a + part].reshape(cells_x * kc, 128) for part in range(2) for h in range(halves)
            ]
            pair = split(jnp.concatenate(parts, axis=1))
            res = three_pass(pair, (vy_h[...], vy_l[...]), dims)
            for part in range(2):
                piece = res[:, part * cells_y:(part + 1) * cells_y].reshape(cells_x, kc, cells_y)
                out_u[:, 2 * a + part, j * kc:(j + 1) * kc, :] = piece

    for step in range(MATVECS):
        source, image = (pol_ref, first_ref) if step == 0 else (first_ref, second_ref)
        for c in range(3):
            forward_z(c, source[c, 0] * mask_ref[...])
        if step == 0:
            pl.semaphore_wait(barrier, n - 1)
        for j in range(chunks):
            exchange(out_t, in_t, j, fs_sem.at[step, j], fr_sem.at[step, j])
        if step == 0:
            order_green()
        for j in range(chunks):
            drain(in_t, fr_sem.at[step, j], j)
            middle(j)
            exchange(out_u, in_u, j, is_sem.at[step, j], ir_sem.at[step, j])
        for j in range(chunks):
            drain(out_t, fs_sem.at[step, j], j)
        for j in range(chunks):
            drain(in_u, ir_sem.at[step, j], j)
        for a in range(3):
            total = None
            for part in range(2):
                rows = slice(part * 2 * cells_z, (part + 1) * 2 * cells_z)
                field = in_u[:, 2 * a + part].reshape(2 * cells_z, cells_y)
                dims = (((0,), (0,)), ((), ()))
                term = three_pass(split(field), (vz_h[rows, :], vz_l[rows, :]), dims)
                total = term if total is None else total + term
            masked = source[a, 0] * mask_ref[...]
            image[a, 0] = inv_ref[0] * masked - mask_ref[...] * total
        for j in range(chunks):
            drain(out_u, is_sem.at[step, j], j)


def per_device(n, polarization, inverse_polarizability, occupancy, green_fourier):
    _, _, cells_y, cells_z = polarization.shape
    _, kz_own, padded_x, padded_y = green_fourier.shape
    padded_z = 2 * cells_z
    cells_x = padded_x // 2
    kc = min(8, kz_own)
    chunks = kz_own // kc
    halves = padded_y // 128
    cos, sin = tables(padded_z, cells_z, padded_z)
    wz = split_table(np.concatenate([cos, -sin], axis=0))
    cos, sin = tables(cells_y, padded_y, padded_y)
    wy = split_table(np.block([[cos, -sin], [sin, cos]]))
    cos, sin = tables(padded_y, cells_y, padded_y)
    vy = split_table(np.block([[cos, sin], [-sin, cos]]))
    cos, sin = tables(padded_z, cells_z, padded_z)
    vz = split_table(np.concatenate([cos, -sin], axis=0) / (padded_x * padded_y * padded_z))
    vmem = pl.BlockSpec(memory_space=pltpu.VMEM)
    sems = pltpu.SemaphoreType.DMA((MATVECS, chunks))
    return pl.pallas_call(
        functools.partial(kernel, n, cells_x, padded_x, kz_own, kc),
        out_shape=(jax.ShapeDtypeStruct(polarization.shape, F32),) * 2,
        in_specs=[vmem] * 3 + [pl.BlockSpec(memory_space=pl.ANY)] + [vmem] * 8,
        out_specs=(vmem, vmem),
        scratch_shapes=[
            pltpu.VMEM(green_fourier.shape, F32),
            pltpu.VMEM((chunks, halves, 6, padded_x, kc, 128), F32),
            pltpu.VMEM((cells_y, cells_z), F32),
            pltpu.VMEM((n, 6, kz_own, cells_y), F32),
            pltpu.VMEM((n, 6, kz_own, cells_y), F32),
            pltpu.VMEM((halves, 6, cells_x, kc, 128), F32),
            pltpu.VMEM((6, padded_x, kc, 128), F32),
            pltpu.VMEM((n, 6, kz_own, cells_y), F32),
            pltpu.VMEM((n, 6, kz_own, cells_y), F32),
            pltpu.SemaphoreType.DMA,
            sems, sems, sems, sems,
        ],
        compiler_params=pltpu.CompilerParams(
            collective_id=0, has_side_effects=True, vmem_limit_bytes=60 * 1024 * 1024
        ),
    )(polarization, inverse_polarizability, occupancy, green_fourier, *map(jnp.asarray, wz + wy + vy + vz))


def solution(mesh):
    return jax.shard_map(
        functools.partial(per_device, mesh.shape["slab"]),
        mesh=mesh,
        in_specs=(
            P("comp", "slab", None, None),
            P("slab", None, None),
            P("slab", None, None),
            P(None, "slab", None, None),
        ),
        out_specs=(P("comp", "slab", None, None), P("comp", "slab", None, None)),
        check_vma=False,
    )
```

profile of v0, /device:TPU:0, one launch (start us, length us, event | category | flops | bytes accessed | tf_op | source)
XLA Modules:
  0.0 85.1 jit_solution(4961587637323646351)
XLA Ops:
  0.6 81.2 %shard_map.131 = (f32[3,1,128,128]{3,2,1,0:T(8,128)}, f32[3,1,128,128]{3,2,1,0:T(8,128)}) custom-call(f32[3,1,128,128]{3,2,1,0:T(8,128)} %pol_ref.1, f32[1,128,128]{2,1,0:T(8,128)} %inv_ref.1, s32[1,16,16]{2,1,0:T(8,128)} %occ_ref.1, f32[6,16,32,256]{3,2,1,0:T(8,128)} %green_ref.1, bf16[512,128]{1,0:T(8,128)(2,1)} %constant.16.clone.wz_h, ...), custom_call_target="tpu_custom_call" | custom-call | tf_op jit(solution)/shard_map/pallas_call | solution.py:252
  81.9 1.6 %copy.16 = f32[3,1,128,128]{3,2,1,0:T(8,128)} copy(f32[3,1,128,128]{3,2,1,0:T(8,128)} %get-tuple-element.4) | data formatting | bytes 393216
  83.5 1.6 %copy.17 = f32[3,1,128,128]{3,2,1,0:T(8,128)} copy(f32[3,1,128,128]{3,2,1,0:T(8,128)} %get-tuple-element.5) | data formatting | bytes 393216
where the time goes:
time: 85.3 us; the launch traced here: 85.1 us
  Pallas kernels  81.2 us (95%)
  local copies, waits for them, and re-layouts  3.23 us (4%)
    pallas_call x1, Pallas kernels, per_device(): pl.pallas_call(functools.partial(kernel, n, cells_x, padded_x, kz_own, kc...  81.2 us
    unnamed x2, local copies, waits for them, and re-layouts  3.23 us

commit v1 on v0

v1 whole, which is shorter than its diff:
```python
import functools
import math

import jax
import jax.numpy as jnp
import numpy as np
from jax import lax
from jax.experimental import pallas as pl
from jax.experimental.pallas import tpu as pltpu
from jax.sharding import PartitionSpec as P

BLOCK = 8
MATVECS = 2
F32 = jnp.float32
BF16 = jnp.bfloat16
COMBOS = ((0, 3, 4), (3, 1, 5), (4, 5, 2))


def tables(count_in, count_out, length):
    phase = np.arange(count_in)[:, None] * np.arange(count_out)[None, :] % length
    angle = phase * (2.0 * math.pi / length)
    return np.cos(angle), np.sin(angle)


def split_table(table):
    table = table.astype(np.float32)
    high = table.astype(jnp.bfloat16)
    low = (table - high.astype(np.float32)).astype(jnp.bfloat16)
    return high, low


def split(value):
    high = value.astype(BF16)
    return high, (value - high.astype(F32)).astype(BF16)


def twiddle(re, im, num, length, sign):
    num = num * sign % length
    if num == 0:
        return re, im
    if 4 * num == length:
        return -im, re
    if 2 * num == length:
        return -re, -im
    if 4 * num == 3 * length:
        return im, -re
    c = math.cos(2.0 * math.pi * num / length)
    s = math.sin(2.0 * math.pi * num / length)
    if (8 * num) % length == 0:
        a = abs(c)
        p, m = (re + im) * a, (re - im) * a
        return {1: (m, p), 3: (-p, m), 5: (-m, -p), 7: (p, -m)}[8 * num // length]
    return re * c - im * s, re * s + im * c


def fft(values, sign):
    n = len(values)
    if n == 1:
        return values
    even, odd = fft(values[0::2], sign), fft(values[1::2], sign)
    low, high = [], []
    for k in range(n // 2):
        (er, ei), (o_r, oi) = even[k], twiddle(*odd[k], k, n, sign)
        low.append((er + o_r, ei + oi))
        high.append((er - o_r, ei - oi))
    return low + high


def three_pass(pair, table_pair, dims):
    dot = functools.partial(lax.dot_general, dimension_numbers=dims, preferred_element_type=F32)
    (vh, vl), (th, tl) = pair, table_pair
    return dot(vh, th) + (dot(vl, th) + dot(vh, tl))


def kernel(
    n, cells_x, padded_x, kz_own, kc,
    pol_ref, inv_ref, occ_ref, green_ref, wz_h, wz_l, wy_h, wy_l, vy_h, vy_l, vz_h, vz_l,
    first_ref, second_ref,
    green_raw, green, mask_ref, raw_out, raw_in, out_t, in_t, lines, spec, out_u, in_u, part_out, part_in,
    green_sem, ws_sem, wr_sem, ts_sem, tr_sem, cs_sem, cr_sem, os_sem, or_sem, ps_sem, pr_sem,
):
    me = lax.axis_index("slab")
    group = n // 2
    here = me // group
    seat = lax.rem(me, group)
    twin = lax.rem(me + group, n)
    base = here * group
    chunks = kz_own // kc
    cells_y, cells_z = mask_ref.shape
    padded_y = 2 * cells_y
    halves = padded_y // 128
    kz_half = group * kz_own
    green_copy = pltpu.make_async_copy(green_ref, green_raw, green_sem)
    green_copy.start()

    def signal(device):
        pl.semaphore_signal(barrier, inc=1, device_id={"slab": device}, device_id_type=pl.DeviceIdType.MESH)

    def remote(source, target, send_sem, recv_sem, device):
        return pltpu.make_async_remote_copy(
            src_ref=source, dst_ref=target, send_sem=send_sem, recv_sem=recv_sem,
            device_id={"slab": device}, device_id_type=pl.DeviceIdType.MESH,
        )

    barrier = pltpu.get_barrier_semaphore()
    signal(twin)

    def greet(k, carry):
        signal(base + lax.rem(seat + k, group))
        return carry

    lax.fori_loop(1, group, greet, 0)

    blocks_y, blocks_z = occ_ref.shape[1:]
    up_y = lax.broadcasted_iota(jnp.int32, (cells_y, blocks_y), 0) // BLOCK
    up_y = (up_y == lax.broadcasted_iota(jnp.int32, (cells_y, blocks_y), 1)).astype(F32).astype(BF16)
    up_z = lax.broadcasted_iota(jnp.int32, (blocks_z, cells_z), 1) // BLOCK
    up_z = (up_z == lax.broadcasted_iota(jnp.int32, (blocks_z, cells_z), 0)).astype(F32).astype(BF16)
    flags = occ_ref[0].astype(F32).astype(BF16)
    spread = jnp.dot(up_y, flags, preferred_element_type=F32).astype(BF16)
    mask_ref[...] = jnp.dot(spread, up_z, preferred_element_type=F32)

    def order_green():
        green_copy.wait()

        def one(g, carry):
            for j in range(chunks):
                for t in range(0, padded_x, 8):
                    tile = green_raw[g, j * kc:(j + 1) * kc, t:t + 8, :]
                    tile = jnp.swapaxes(tile, 0, 1)
                    for h in range(halves):
                        green[j * halves + h, g, t:t + 8] = tile[:, :, h * 128:(h + 1) * 128]
            return carry

        lax.fori_loop(0, 6, one, 0)

    def send_raw(step, c, field):
        raw_out[c] = field
        remote(raw_out.at[c], raw_in.at[c], ws_sem.at[step, c], wr_sem.at[step, c], twin).start()

    def forward_z(step, c, which, field):
        pair = split(field)
        slab = me if which == 0 else twin
        for part in range(2):
            dims = (((1,), (1,)), ((), ()))
            res = three_pass((wz_h[here, part], wz_l[here, part]), pair, dims)
            out_t[c, which, :, part] = res.reshape(group, kz_own, cells_y)

        def send(k, carry):
            to = lax.rem(seat + k, group)
            remote(
                out_t.at[c, which, to], in_t.at[c, slab], ts_sem.at[step, c], tr_sem.at[step, c], base + to
            ).start()
            return carry

        lax.fori_loop(1, group, send, 0)
        in_t[c, slab] = out_t[c, which, seat]

    def drain(view, sem):
        pltpu.make_async_copy(view, view, sem).wait()

    def forward_yx(step, c):
        drain(in_t.at[c, pl.ds(0, n - 2)], tr_sem.at[step, c])
        parts = [in_t[c, :, part].reshape(cells_x * kz_own, cells_y) for part in range(2)]
        dims = (((1,), (0,)), ((), ()))
        res = three_pass(split(jnp.concatenate(parts, axis=1)), (wy_h[...], wy_l[...]), dims)
        for part in range(2):
            for h in range(halves):
                at = part * padded_y + h * 128
                piece = res[:, at:at + 128].reshape(cells_x, kz_own, 128)
                for j in range(chunks):
                    lines[j * halves + h, part] = piece[:, j * kc:(j + 1) * kc]

        def columns(i, carry):
            line = [(lines[i, 0, x], lines[i, 1, x]) for x in range(cells_x)]
            for m, (re, im) in enumerate(fft(line, -1)):
                spec[i, 2 * c, 2 * m], spec[i, 2 * c + 1, 2 * m] = re, im
            line = [twiddle(lines[i, 0, x], lines[i, 1, x], x, padded_x, -1) for x in range(cells_x)]
            for m, (re, im) in enumerate(fft(line, -1)):
                spec[i, 2 * c, 2 * m + 1], spec[i, 2 * c + 1, 2 * m + 1] = re, im
            return carry

        lax.fori_loop(0, chunks * halves, columns, 0)

    def backward_xy(step, a):
        row = COMBOS[a]

        def columns(i, carry):
            def field(k):
                g = [green[i, r, k] for r in row]
                s = [spec[i, r, k] for r in range(6)]
                return g[0] * s[0] + g[1] * s[2] + g[2] * s[4], g[0] * s[1] + g[1] * s[3] + g[2] * s[5]

            even = fft([field(k) for k in range(0, padded_x, 2)], 1)
            for x in range(cells_x):
                lines[i, 0, x], lines[i, 1, x] = even[x]
            odd = fft([field(k) for k in range(1, padded_x, 2)], 1)
            for x in range(cells_x):
                re, im = twiddle(*odd[x], x, padded_x, 1)
                lines[i, 0, x] += re
                lines[i, 1, x] += im
            return carry

        lax.fori_loop(0, chunks * halves, columns, 0)
        parts = []
        for part in range(2):
            for h in range(halves):
                pieces = [lines[j * halves + h, part] for j in range(chunks)]
                piece = pieces[0] if chunks == 1 else jnp.concatenate(pieces, axis=1)
                parts.append(piece.reshape(cells_x * kz_own, 128))
        dims = (((1,), (0,)), ((), ()))
        res = three_pass(split(jnp.concatenate(parts, axis=1)), (vy_h[...], vy_l[...]), dims)
        for part in range(2):
            piece = res[:, part * cells_y:(part + 1) * cells_y]
            out_u[a, :, part] = piece.reshape(cells_x, kz_own, cells_y)
        there = (1 - here) * group
        for which, first, s_sem, r_sem in ((1, there, cs_sem, cr_sem), (0, base, os_sem, or_sem)):

            def send(k, carry):
                to = lax.rem(seat + k, group)
                remote(
                    out_u.at[a, first + to], in_u.at[a, which, seat], s_sem.at[step, a], r_sem.at[step, a], base + to
                ).start()
                return carry

            lax.fori_loop(1, group, send, 0)
            in_u[a, which, seat] = out_u[a, first + seat]

    def inverse_z(a, which):
        total = None
        for part in range(2):
            field = in_u[a, which, :, part].reshape(kz_half, cells_y)
            dims = (((0,), (0,)), ((), ()))
            term = three_pass(split(field), (vz_h[here, part], vz_l[here, part]), dims)
            total = term if total is None else total + term
        return total

    def send_part(step, a):
        drain(in_u.at[a, 1, pl.ds(0, group - 1)], cr_sem.at[step, a])
        part_out[a] = inverse_z(a, 1)
        remote(part_out.at[a], part_in.at[a], ps_sem.at[step, a], pr_sem.at[step, a], twin).start()

    for step in range(MATVECS):
        source, image = (pol_ref, first_ref) if step == 0 else (first_ref, second_ref)
        if step == 0:
            pl.semaphore_wait(barrier, group)
            for c in range(3):
                send_raw(step, c, source[c, 0] * mask_ref[...])
            for c in range(3):
                forward_z(step, c, 0, raw_out[c])
            order_green()
        for c in range(3):
            drain(raw_in.at[c], wr_sem.at[step, c])
            forward_z(step, c, 1, raw_in[c])
            if c > 0:
                forward_yx(step, c - 1)
        forward_yx(step, 2)
        for a in range(3):
            backward_xy(step, a)
            if a > 0:
                send_part(step, a - 1)
        send_part(step, 2)
        for c in range(3):
            drain(raw_out.at[c], ws_sem.at[step, c])
            drain(in_t.at[c, pl.ds(0, n - 2)], ts_sem.at[step, c])
        for a in range(3):
            drain(in_u.at[a, 0, pl.ds(0, group - 1)], or_sem.at[step, a])
            own = inverse_z(a, 0)
            masked = source[a, 0] * mask_ref[...]
            drain(part_in.at[a], pr_sem.at[step, a])
            image[a, 0] = inv_ref[0] * masked - mask_ref[...] * (own + part_in[a])
            if step + 1 < MATVECS:
                send_raw(step + 1, a, image[a, 0] * mask_ref[...])
                forward_z(step + 1, a, 0, raw_out[a])
        for a in range(3):
            drain(in_u.at[a, 1, pl.ds(0, group - 1)], cs_sem.at[step, a])
            drain(in_u.at[a, 0, pl.ds(0, group - 1)], os_sem.at[step, a])
            drain(part_out.at[a], ps_sem.at[step, a])


def per_device(n, polarization, inverse_polarizability, occupancy, green_fourier):
    _, _, cells_y, cells_z = polarization.shape
    _, kz_own, padded_x, padded_y = green_fourier.shape
    padded_z = 2 * cells_z
    cells_x = padded_x // 2
    kc = min(8, kz_own)
    chunks = kz_own // kc
    halves = padded_y // 128
    cos, sin = tables(padded_z, cells_z, padded_z)
    wz = split_table(np.stack([cos, -sin]).reshape(2, 2, cells_z, cells_z).swapaxes(0, 1))
    cos, sin = tables(cells_y, padded_y, padded_y)
    wy = split_table(np.block([[cos, -sin], [sin, cos]]))
    cos, sin = tables(padded_y, cells_y, padded_y)
    vy = split_table(np.block([[cos, sin], [-sin, cos]]))
    cos, sin = tables(padded_z, cells_z, padded_z)
    vz = np.stack([cos, -sin]).reshape(2, 2, cells_z, cells_z).swapaxes(0, 1)
    vz = split_table(vz / (padded_x * padded_y * padded_z))
    vmem = pl.BlockSpec(memory_space=pltpu.VMEM)
    return pl.pallas_call(
        functools.partial(kernel, n, cells_x, padded_x, kz_own, kc),
        out_shape=(jax.ShapeDtypeStruct(polarization.shape, F32),) * 2,
        in_specs=[vmem] * 3 + [pl.BlockSpec(memory_space=pl.ANY)] + [vmem] * 8,
        out_specs=(vmem, vmem),
        scratch_shapes=[
            pltpu.VMEM(green_fourier.shape, F32),
            pltpu.VMEM((chunks * halves, 6, padded_x, kc, 128), F32),
            pltpu.VMEM((cells_y, cells_z), F32),
            pltpu.VMEM((3, cells_y, cells_z), F32),
            pltpu.VMEM((3, cells_y, cells_z), F32),
            pltpu.VMEM((3, 2, n // 2, 2, kz_own, cells_y), F32),
            pltpu.VMEM((3, n, 2, kz_own, cells_y), F32),
            pltpu.VMEM((chunks * halves, 2, cells_x, kc, 128), F32),
            pltpu.VMEM((chunks * halves, 6, padded_x, kc, 128), F32),
            pltpu.VMEM((3, n, 2, kz_own, cells_y), F32),
            pltpu.VMEM((3, 2, n // 2, 2, kz_own, cells_y), F32),
            pltpu.VMEM((3, cells_y, cells_z), F32),
            pltpu.VMEM((3, cells_y, cells_z), F32),
            pltpu.SemaphoreType.DMA,
            *[pltpu.SemaphoreType.DMA((MATVECS, 3))] * 10,
        ],
        compiler_params=pltpu.CompilerParams(
            collective_id=0, has_side_effects=True, vmem_limit_bytes=60 * 1024 * 1024
        ),
    )(polarization, inverse_polarizability, occupancy, green_fourier, *map(jnp.asarray, wz + wy + vy + vz))


def solution(mesh):
    return jax.shard_map(
        functools.partial(per_device, mesh.shape["slab"]),
        mesh=mesh,
        in_specs=(
            P("comp", "slab", None, None),
            P("slab", None, None),
            P("slab", None, None),
            P(None, "slab", None, None),
        ),
        out_specs=(P("comp", "slab", None, None), P("comp", "slab", None, None)),
        check_vma=False,
    )
```

time: 85.3 us -> 77.2 us (0.905)
  Pallas kernels: 81.2 us -> 73.1 us
    pallas_call x1, Pallas kernels: 81.2 us -> 73.1 us  [per_device(): pl.pallas_call(functools.partial(kernel, n, cells_x, padded_x, kz_own, kc...]
where the time goes in v1:
time: 77.2 us; the launch traced here: 77 us
  Pallas kernels  73.1 us (95%)
  local copies, waits for them, and re-layouts  3.23 us (4%)
    pallas_call x1, Pallas kernels, per_device(): pl.pallas_call(functools.partial(kernel, n, cells_x, padded_x, kz_own, kc...  73.1 us
    unnamed x2, local copies, waits for them, and re-layouts  3.23 us

profile of v1, /device:TPU:0, one launch (start us, length us, event | category | flops | bytes accessed | tf_op | source)
XLA Modules:
  0.0 77.0 jit_solution(10318663801364084788)
XLA Ops:
  0.6 73.1 %shard_map.131 = (f32[3,1,128,128]{3,2,1,0:T(8,128)}, f32[3,1,128,128]{3,2,1,0:T(8,128)}) custom-call(f32[3,1,128,128]{3,2,1,0:T(8,128)} %pol_ref.1, f32[1,128,128]{2,1,0:T(8,128)} %inv_ref.1, s32[1,16,16]{2,1,0:T(8,128)} %occ_ref.1, f32[6,16,32,256]{3,2,1,0:T(8,128)} %green_ref.1, bf16[2,2,128,128]{3,2,1,0:T(8,128)(2,1)} %constant.16.clone.wz_h, ...), custom_call_target="tpu_custom_call" | custom-call | tf_op jit(solution)/shard_map/pallas_call | solution.py:299
  73.7 1.6 %copy.16 = f32[3,1,128,128]{3,2,1,0:T(8,128)} copy(f32[3,1,128,128]{3,2,1,0:T(8,128)} %get-tuple-element.4) | data formatting | bytes 393216
  75.4 1.6 %copy.17 = f32[3,1,128,128]{3,2,1,0:T(8,128)} copy(f32[3,1,128,128]{3,2,1,0:T(8,128)} %get-tuple-element.5) | data formatting | bytes 393216

commit v2 on v1

--- a/solution.py
+++ b/solution.py
@@ -213,18 +213,18 @@
         for part in range(2):
             piece = res[:, part * cells_y:(part + 1) * cells_y]
             out_u[a, :, part] = piece.reshape(cells_x, kz_own, cells_y)
-        there = (1 - here) * group
-        for which, first, s_sem, r_sem in ((1, there, cs_sem, cr_sem), (0, base, os_sem, or_sem)):
-
-            def send(k, carry):
-                to = lax.rem(seat + k, group)
-                remote(
-                    out_u.at[a, first + to], in_u.at[a, which, seat], s_sem.at[step, a], r_sem.at[step, a], base + to
-                ).start()
-                return carry
-
-            lax.fori_loop(1, group, send, 0)
-            in_u[a, which, seat] = out_u[a, first + seat]
+        send_back(step, a, 1, (1 - here) * group, cs_sem, cr_sem)
+
+    def send_back(step, a, which, first, s_sem, r_sem):
+        def send(k, carry):
+            to = lax.rem(seat + k, group)
+            remote(
+                out_u.at[a, first + to], in_u.at[a, which, seat], s_sem.at[step, a], r_sem.at[step, a], base + to
+            ).start()
+            return carry
+
+        lax.fori_loop(1, group, send, 0)
+        in_u[a, which, seat] = out_u[a, first + seat]
 
     def inverse_z(a, which):
         total = None
@@ -257,8 +257,11 @@
         forward_yx(step, 2)
         for a in range(3):
             backward_xy(step, a)
-            if a > 0:
-                send_part(step, a - 1)
+            if a == 1:
+                send_part(step, 0)
+        for a in range(3):
+            send_back(step, a, 0, base, os_sem, or_sem)
+        send_part(step, 1)
         send_part(step, 2)
         for c in range(3):
             drain(raw_out.at[c], ws_sem.at[step, c])
@@ -276,6 +279,24 @@
             drain(in_u.at[a, 1, pl.ds(0, group - 1)], cs_sem.at[step, a])
             drain(in_u.at[a, 0, pl.ds(0, group - 1)], os_sem.at[step, a])
             drain(part_out.at[a], ps_sem.at[step, a])
+
+
+def deliver(first_ref, second_ref, first_out, second_out, first, second, in_sem, out_sem):
+    loads = [
+        pltpu.make_async_copy(source, held, in_sem.at[i])
+        for i, (source, held) in enumerate(((first_ref, first), (second_ref, second)))
+    ]
+    stores = [
+        pltpu.make_async_copy(held, target, out_sem.at[i])
+        for i, (held, target) in enumerate(((first, first_out), (second, second_out)))
+    ]
+    for copy in loads:
+        copy.start()
+    for load, store in zip(loads, stores):
+        load.wait()
+        store.start()
+    for store in stores:
+        store.wait()
 
 
 def per_device(n, polarization, inverse_polarizability, occupancy, green_fourier):
@@ -296,7 +317,7 @@
     vz = np.stack([cos, -sin]).reshape(2, 2, cells_z, cells_z).swapaxes(0, 1)
     vz = split_table(vz / (padded_x * padded_y * padded_z))
     vmem = pl.BlockSpec(memory_space=pltpu.VMEM)
-    return pl.pallas_call(
+    images = pl.pallas_call(
         functools.partial(kernel, n, cells_x, padded_x, kz_own, kc),
         out_shape=(jax.ShapeDtypeStruct(polarization.shape, F32),) * 2,
         in_specs=[vmem] * 3 + [pl.BlockSpec(memory_space=pl.ANY)] + [vmem] * 8,
@@ -322,6 +343,14 @@
             collective_id=0, has_side_effects=True, vmem_limit_bytes=60 * 1024 * 1024
         ),
     )(polarization, inverse_polarizability, occupancy, green_fourier, *map(jnp.asarray, wz + wy + vy + vz))
+    anywhere = pl.BlockSpec(memory_space=pl.ANY)
+    return pl.pallas_call(
+        deliver,
+        out_shape=(jax.ShapeDtypeStruct(polarization.shape, F32),) * 2,
+        in_specs=[anywhere] * 2,
+        out_specs=(anywhere, anywhere),
+        scratch_shapes=[pltpu.VMEM(polarization.shape, F32)] * 2 + [pltpu.SemaphoreType.DMA((2,))] * 2,
+    )(*images)
 
 
 def solution(mesh):

time: 77.2 us -> 77.4 us (level)
  Pallas kernels: 73.1 us -> 76.6 us
  local copies, waits for them, and re-layouts: 3.23 us -> 0 us
    unnamed x2 -> x0, local copies, waits for them, and re-layouts: 3.23 us -> none
    pallas_call x1, Pallas kernels: 73.1 us -> 74.9 us  [per_device(): pl.pallas_call(functools.partial(kernel, n, cells_x, padded_x, kz_own, kc...]
    pallas_call x0 -> x1, Pallas kernels: none -> 1.73 us  [per_device(): pl.pallas_call(deliver, out_shape=(jax.ShapeDtypeStruct(polarization.shap...]
where the time goes in v2:
time: 77.4 us; the launch traced here: 77.2 us
  Pallas kernels  76.6 us (99%)
    pallas_call x1, Pallas kernels, per_device(): pl.pallas_call(functools.partial(kernel, n, cells_x, padded_x, kz_own, kc...  74.9 us
    pallas_call x1, Pallas kernels, per_device(): pl.pallas_call(deliver, out_shape=(jax.ShapeDtypeStruct(polarization.shap...  1.73 us

profile of v2, /device:TPU:0, one launch (start us, length us, event | category | flops | bytes accessed | tf_op | source)
XLA Modules:
  0.0 77.2 jit_solution(4538708287135868436)
XLA Ops:
  0.6 74.9 %shard_map.131 = (f32[3,1,128,128]{3,2,1,0:T(8,128)}, f32[3,1,128,128]{3,2,1,0:T(8,128)}) custom-call(f32[3,1,128,128]{3,2,1,0:T(8,128)} %pol_ref.1, f32[1,128,128]{2,1,0:T(8,128)} %inv_ref.1, s32[1,16,16]{2,1,0:T(8,128)} %occ_ref.1, f32[6,16,32,256]{3,2,1,0:T(8,128)} %green_ref.1, bf16[2,2,128,128]{3,2,1,0:T(8,128)(2,1)} %constant.16.clone.wz_h, ...), custom_call_target="tpu_custom_call" | custom-call | tf_op jit(solution)/shard_map/pallas_call | solution.py:320
  75.5 1.7 %shard_map.132 = (f32[3,1,128,128]{3,2,1,0:T(8,128)}, f32[3,1,128,128]{3,2,1,0:T(8,128)}) custom-call(f32[3,1,128,128]{3,2,1,0:T(8,128)} %get-tuple-element.4.first_ref, f32[3,1,128,128]{3,2,1,0:T(8,128)} %get-tuple-element.5.second_ref), custom_call_target="tpu_custom_call" | custom-call | tf_op jit(solution)/shard_map/pallas_call | solution.py:347

commit v3 on v2

--- a/solution.py
+++ b/solution.py
@@ -214,6 +214,7 @@
             piece = res[:, part * cells_y:(part + 1) * cells_y]
             out_u[a, :, part] = piece.reshape(cells_x, kz_own, cells_y)
         send_back(step, a, 1, (1 - here) * group, cs_sem, cr_sem)
+        send_back(step, a, 0, base, os_sem, or_sem)
 
     def send_back(step, a, which, first, s_sem, r_sem):
         def send(k, carry):
@@ -257,11 +258,8 @@
         forward_yx(step, 2)
         for a in range(3):
             backward_xy(step, a)
-            if a == 1:
-                send_part(step, 0)
-        for a in range(3):
-            send_back(step, a, 0, base, os_sem, or_sem)
-        send_part(step, 1)
+            if a > 0:
+                send_part(step, a - 1)
         send_part(step, 2)
         for c in range(3):
             drain(raw_out.at[c], ws_sem.at[step, c])

time: 77.4 us -> 76.5 us (0.988)
  Pallas kernels: 76.6 us -> 75.7 us
    pallas_call x1, Pallas kernels: 74.9 us -> 73.9 us  [per_device(): pl.pallas_call(functools.partial(kernel, n, cells_x, padded_x, kz_own, kc...]
where the time goes in v3:
time: 76.5 us; the launch traced here: 76.3 us
  Pallas kernels  75.7 us (99%)
    pallas_call x1, Pallas kernels, per_device(): pl.pallas_call(functools.partial(kernel, n, cells_x, padded_x, kz_own, kc...  73.9 us
    pallas_call x1, Pallas kernels, per_device(): pl.pallas_call(deliver, out_shape=(jax.ShapeDtypeStruct(polarization.shap...  1.73 us

profile of v3, /device:TPU:0, one launch (start us, length us, event | category | flops | bytes accessed | tf_op | source)
XLA Modules:
  0.0 76.3 jit_solution(289845532816997189)
XLA Ops:
  0.6 73.9 %shard_map.131 = (f32[3,1,128,128]{3,2,1,0:T(8,128)}, f32[3,1,128,128]{3,2,1,0:T(8,128)}) custom-call(f32[3,1,128,128]{3,2,1,0:T(8,128)} %pol_ref.1, f32[1,128,128]{2,1,0:T(8,128)} %inv_ref.1, s32[1,16,16]{2,1,0:T(8,128)} %occ_ref.1, f32[6,16,32,256]{3,2,1,0:T(8,128)} %green_ref.1, bf16[2,2,128,128]{3,2,1,0:T(8,128)(2,1)} %constant.16.clone.wz_h, ...), custom_call_target="tpu_custom_call" | custom-call | tf_op jit(solution)/shard_map/pallas_call | solution.py:318
  74.6 1.7 %shard_map.132 = (f32[3,1,128,128]{3,2,1,0:T(8,128)}, f32[3,1,128,128]{3,2,1,0:T(8,128)}) custom-call(f32[3,1,128,128]{3,2,1,0:T(8,128)} %get-tuple-element.4.first_ref, f32[3,1,128,128]{3,2,1,0:T(8,128)} %get-tuple-element.5.second_ref), custom_call_target="tpu_custom_call" | custom-call | tf_op jit(solution)/shard_map/pallas_call | solution.py:345
